TPU v7x, 8 devices: a whole 2x2x1 slice. The times are simulated.
8 devices in a mesh: dp: 1 (over z), dcp: 8 (over y, x, core).
Axes of the slice: x: 2, y: 2, z: 1, core: 2. Of those that a mesh axis runs over, the one named last changes fastest.
Arguments:
- q: bfloat16 [128, 64, 576], P('dp', 'dcp')
- cache: bfloat16 [128, 128, 8, 8, 576], P('dp', None, 'dcp')
- lens: int32 [128], P('dp')
Outputs:
- output: bfloat16 [128, 64, 512], P('dp', 'dcp')
All inputs are finite; a program needn't handle non-finite values.
Results may differ from a plain program's by a relative error of at most 0.00740601.
Values are sent between devices in bfloat16 or wider.
A program may use at most 1 GiB of HBM per device.

v0:
```python
import jax
import jax.numpy as jnp
from jax import lax
from jax.sharding import PartitionSpec as P

ROPE = 64
QK_DIM = 192
SCALE = QK_DIM ** -0.5


def solution(mesh):
    n = mesh.shape['dcp']

    def local(q, cache, lens):
        b, hl, k = q.shape
        r = cache.shape[1]
        page = cache.shape[3]
        lorav = k - ROPE
        d = lax.axis_index('dcp')
        qa = lax.all_gather(q, 'dcp', axis=1, tiled=True)
        c = cache.reshape(b, r * page, k)
        pos = (jnp.arange(r)[:, None] * n + d) * page + jnp.arange(page)[None, :]
        valid = pos.reshape(r * page)[None, :] < lens[:, None]
        s = jnp.einsum('bhk,btk->bht', qa, c, preferred_element_type=jnp.float32) * SCALE
        s = jnp.where(valid[:, None, :], s, -jnp.inf)
        m = jnp.max(s, axis=2)
        m = jnp.where(jnp.isfinite(m), m, 0.0)
        p = jnp.exp(s - m[:, :, None])
        l = jnp.sum(p, axis=2)
        has = l > 0.0
        lsafe = jnp.where(has, l, 1.0)
        pv = jnp.einsum('bht,btk->bhk', p.astype(jnp.bfloat16), c[:, :, :lorav], preferred_element_type=jnp.float32)
        od = (pv / lsafe[:, :, None]).astype(jnp.bfloat16)
        lse = jnp.where(has, m + jnp.log(lsafe), -jnp.inf)
        od = lax.all_to_all(od.reshape(b, n, hl, lorav), 'dcp', 1, 1, tiled=True)
        lse = lax.all_to_all(lse.reshape(b, n, hl), 'dcp', 1, 1, tiled=True)
        top = jnp.max(lse, axis=1)
        w = jnp.exp(lse - top[:, None, :])
        o = jnp.sum(w[:, :, :, None] * od.astype(jnp.float32), axis=1) / jnp.sum(w, axis=1)[:, :, None]
        return o.astype(jnp.bfloat16)

    return jax.shard_map(local, mesh=mesh, in_specs=(P('dp', 'dcp', None), P('dp', None, 'dcp', None, None), P('dp')), out_specs=P('dp', 'dcp', None), check_vma=False)
```

profile of v0, /device:TPU:0, one launch (start us, length us, event | category | flops | bytes accessed | tf_op | source)
XLA Modules:
  0.0 477.8 jit_solution(8500244918116605734)
XLA Ops:
  6.5 0.0 all-gather.2.cloned.1.call-start
  6.5 2.8 copy.13
  9.4 0.0 all-gather.2.cloned.1.call-update
  9.4 0.1 iota_add_fusion
  9.5 0.1 add.40
  9.6 0.0 copy-start
  9.6 197.6 %copy.14 = bf16[128,128,1,8,576]{4,3,1,0,2:T(8,128)(2,1)} copy(bf16[128,128,1,8,576]{1,4,3,2,0:T(8,128)(2,1)} %param.4) | data formatting | bytes 301989888 | tf_op args[1]
  207.2 0.0 copy-done
  207.2 0.1 broadcast_compare_fusion
  207.3 0.0 all-gather.2.cloned.1.call-done
  207.4 77.1 %fusion.2 = (f32[128,64]{1,0:T(8,128)S(1)}, f32[128,64,1024]{2,1,0:T(8,128)}) fusion(pred[128,1024]{1,0:T(8,128)(4,1)S(1)} %broadcast_compare_fusion, bf16[128,64,576]{2,1,0:T(8,128)(2,1)} %all-gather.2.cloned.1.call-done, bf16[128,128,1,8,576]{4,3,1,0,2:T(8,128)(2,1)} %copy.14), kind=kOutput, calls=%fused_computation.4 | convolution fusion | flops 9688834048 | bytes 194150400 | tf_op jit(solution)/shard_map/bhk,btk->bht/dot_general | solution.py:24
  284.5 0.1 copy.17
  284.6 14.9 %fusion.4 = f32[128,64]{1,0:T(8,128)S(1)} fusion(f32[128,64,1024]{2,1,0:T(8,128)} %get-tuple-element.8, f32[128,64]{1,0:T(8,128)S(1)} %is-finite_select_fusion, pred[128,1024]{1,0:T(8,128)(4,1)S(1)} %broadcast_compare_fusion), kind=kLoop, calls=%fused_computation.6 | loop fusion | flops 33546240 | bytes 33751040 | tf_op jit(solution)/shard_map/reduce_sum | solution.py:29
  299.5 0.1 copy.16
  299.6 0.6 compare_select_fusion.1
  300.2 4.3 all-to-all-start
  304.5 54.9 %fusion.14 = bf16[128,8,8,512]{3,2,1,0:T(8,128)(2,1)} fusion(f32[128,64]{1,0:T(8,128)S(1)} %compare_select_fusion, bf16[128,1024,576]{2,1,0:T(8,128)(2,1)} %bitcast, f32[128,64,1024]{2,1,0:T(8,128)} %get-tuple-element.8, f32[128,64]{1,0:T(8,128)S(1)} %is-finite_select_fusion, pred[128,1024]{1,0:T(8,128)(4,1)S(1)} %broadcast_compare_fusion), kind=kOutput, calls=%fused_computation.13 | convolution fusion | flops 8631877632 | bytes 176357376 | tf_op jit(solution)/shard_map/bht,btk->bhk/dot_general | solution.py:32
  359.4 7.4 %copy.19 = bf16[128,8,8,512]{3,2,0,1:T(8,128)(2,1)} copy(bf16[128,8,8,512]{3,2,1,0:T(8,128)(2,1)} %fusion.14) | data formatting | bytes 16777216 | tf_op jit(solution)/shard_map/reshape | solution.py:35
  366.8 0.0 all-to-all-done
  366.8 3.8 all-to-all-start.1
  370.7 0.1 copy.20
  370.8 0.2 copy.18
  371.0 93.6 %all-to-all-done.1 = bf16[128,8,8,512]{3,2,0,1:T(8,128)(2,1)} async-done(((bf16[128,8,8,512]{3,2,0,1:T(8,128)(2,1)}), bf16[128,8,8,512]{3,2,0,1:T(8,128)(2,1)}, u32[]{:S(2)}, u32[]{:S(2)}) %all-to-all-start.1) | async-done | bytes 8388640 | tf_op jit(solution)/shard_map/all_to_all | solution.py:35
  464.6 5.1 %multiply_reduce_fusion = f32[128,8,512]{2,1,0:T(8,128)S(1)} fusion(bf16[128,8,8,512]{3,2,0,1:T(8,128)(2,1)} %all-to-all-done.1, f32[128,8,8]{2,0,1:T(8,128)S(1)} %copy.18), kind=kLoop, calls=%fused_computation.7 | loop fusion | flops 12058624 | bytes 10518528 | tf_op jit(solution)/shard_map/reduce_sum | solution.py:39
  469.7 1.2 divide_convert_fusion.1
  (5 shorter events, 0.1 us)
Async XLA Ops:
  6.5 200.8 %all-gather.2.cloned.1.call-start = ((), (), s32[]{:S(2)}) async-start(), calls=%async_computation.2 | async-start | bytes 11796480 | tf_op jit(solution)/shard_map/all_gather | solution.py:20
  9.6 197.6 %copy-start = (s32[128]{0:T(128)S(1)}, s32[128]{0:T(128)}, u32[]{:S(2)}) copy-start(s32[128]{0:T(128)} %param.5) | copy-start | bytes 1540
  300.2 66.6 %all-to-all-start = ((f32[128,8,8]{0,2,1:T(8,128)}), f32[128,8,8]{0,2,1:T(8,128)S(1)}, u32[]{:S(2)}, u32[]{:S(2)}) async-start(f32[128,8,8]{0,2,1:T(8,128)} %compare_select_fusion.1), calls=%async_computation | async-start | bytes 65536 | tf_op jit(solution)/shard_map/all_to_all | solution.py:36
  366.8 97.8 %all-to-all-start.1 = ((bf16[128,8,8,512]{3,2,0,1:T(8,128)(2,1)}), bf16[128,8,8,512]{3,2,0,1:T(8,128)(2,1)}, u32[]{:S(2)}, u32[]{:S(2)}) async-start(bf16[128,8,8,512]{3,2,0,1:T(8,128)(2,1)} %copy.19), calls=%async_computation.1 | async-start | bytes 16777216 | tf_op jit(solution)/shard_map/all_to_all | solution.py:35
Sparse Core Ops, SparseCore 0:
  9.5 60.0 all-gather.1
where the time goes:
time: 483 us; the launch traced here: 478 us
  local copies, waits for them, and re-layouts  208 us (43%)
  matrix products  132 us (27%)
  waiting for transfers between devices  93.7 us (19%)
  other arithmetic  22.1 us (5%)
  between operations  13.5 us (3%)
  starting transfers between devices  8.06 us (2%)
    unnamed x4, local copies, waits for them, and re-layouts  200 us
    all_to_all x1, waiting for transfers between devices, local(): od = lax.all_to_all(od.reshape(b, n, hl, lorav), 'dcp', 1, 1, tiled=True)  93.6 us
    dot_general x1, matrix products, local(): jnp.einsum('bhk,btk->bht', qa, c, preferred_element_type=jnp.float32)  77.1 us
    dot_general x1, matrix products, local(): jnp.einsum('bht,btk->bhk', p.astype(jnp.bfloat16), c[:, :, :lorav], prefe...  54.9 us
    reduce_sum x1, other arithmetic, local(): l = jnp.sum(p, axis=2)  14.9 us
  transfers between devices with their start and end apart: 3, of which 1 were waited for; matrix products, arithmetic and copies ran while one was open for 55% of the time, Pallas kernels for 0%

commit v1 on v0

v1 whole, which is shorter than its diff:
```python
import functools

import jax
import jax.numpy as jnp
from jax import lax
from jax.experimental import pallas as pl
from jax.experimental.pallas import tpu as pltpu
from jax.sharding import PartitionSpec as P

ROPE = 64
QK_DIM = 192
SCALE = QK_DIM ** -0.5
MESH = pl.DeviceIdType.MESH

G = 8
PAIRS = G // 2
AHEAD = 4
LAG1, LAG2, LAG3 = 6, 14, 22
NBUF = 6
AG_KINDS, RS_KINDS = 7, 6


def attend(q, c, length, d, lora):
    heads = q.shape[0]
    slots, k, pages = c.shape
    lane = lax.broadcasted_iota(jnp.int32, (heads, pages), 1)
    s = []
    for i in range(0, slots, 2):
        both = jnp.concatenate([c[i], c[i + 1]], axis=1)
        dots = jnp.dot(q, both, preferred_element_type=jnp.float32)
        for u in range(2):
            n = lax.shift_right_arithmetic(length - slots * d - (i + u) + (slots * 8 - 1), 6)
            s.append(jnp.where(lane < n, dots[:, pages * u:pages * (u + 1)] * SCALE, -jnp.inf))
    m = jnp.max(functools.reduce(jnp.maximum, s), axis=1, keepdims=True)
    m = jnp.where(m == -jnp.inf, 0.0, m)
    p = [jnp.exp(x - m) for x in s]
    l = jnp.sum(functools.reduce(jnp.add, p), axis=1, keepdims=True)
    o = None
    for i in range(0, slots, 2):
        pb = jnp.concatenate([p[i], p[i + 1]], axis=1).astype(jnp.bfloat16)
        both = jnp.concatenate([c[i, :lora], c[i + 1, :lora]], axis=1)
        x = lax.dot_general(pb, both, (((1,), (1,)), ((), ())), preferred_element_type=jnp.float32)
        o = x if o is None else o + x
    has = l > 0.0
    r = jnp.where(has, 1.0 / jnp.where(has, l, 1.0), 0.0)
    lse = jnp.where(has, m + jnp.log(jnp.where(has, l, 1.0)), -jnp.inf)
    return (o * r).astype(jnp.bfloat16), lse


def column(ref, lane, j):
    return jnp.max(jnp.where(lane == j, ref, -jnp.inf), axis=1, keepdims=True)


def merge(oa, la, ob, lb):
    top = jnp.maximum(la, lb)
    top = jnp.where(top == -jnp.inf, 0.0, top)
    wa, wb = jnp.exp(la - top), jnp.exp(lb - top)
    w = wa + wb
    has = w > 0.0
    safe = jnp.where(has, w, 1.0)
    inv = jnp.where(has, 1.0 / safe, 0.0)
    o = (wa * inv) * oa.astype(jnp.float32) + (wb * inv) * ob.astype(jnp.float32)
    return o.astype(jnp.bfloat16), jnp.where(has, top + jnp.log(safe), -jnp.inf)


def kernel(n_seq, lora, lens_ref, q_ref, c_ref, out_ref, kv, qg, o, lse, r1, rl1, r2, rl2, r3, rl3,
           kv_sem, q_sem, send_sem, recv_sem):
    n_groups, n_pairs = n_seq // G, n_seq // 2
    off_pair, off_group = LAG3 + 2, (LAG3 + 2) // PAIRS
    me = lax.axis_index("dcp")
    dp = lax.axis_index("dp")
    y, x, core = me // 4, (me // 2) % 2, me % 2
    partner = (dp, y * 4 + x * 2 + (1 - core))

    def neighbour(g, first):
        par = g % 2 if first else (g + 1) % 2
        return (dp, ((y + par) % 2) * 4 + ((x + 1 - par) % 2) * 2 + core)

    def remote(kind, g, src, dst, device):
        return pltpu.make_async_remote_copy(
            src_ref=src, dst_ref=dst, send_sem=send_sem.at[kind, g], recv_sem=recv_sem.at[kind, g],
            device_id=device, device_id_type=MESH)

    def q_block(g, block):
        return qg.at[pl.ds(g * G, G), pl.ds(block * 8, 8)]

    def q_copy(kind, g):
        src, dst, to = ((0, 4, partner), (0, 2, neighbour(g, True)), (0, 1, neighbour(g, False)),
                        (2, 3, neighbour(g, False)), (2, 6, partner), (1, 5, partner), (3, 7, partner))[kind]
        return remote(kind, g, q_block(g, src), q_block(g, dst), to)

    def seqs(ref, g, lo, hi):
        return ref.at[pl.ds((g + off_group) * G, G), pl.ds(lo, hi - lo)]

    def rs_copies(stage, g):
        rows, dst, ldst, to = ((32, r1, rl1, partner), (16, r2, rl2, neighbour(g, True)),
                               (8, r3, rl3, neighbour(g, False)))[stage]
        kind = AG_KINDS + 2 * stage
        return (remote(kind, g, seqs(o, g, rows, 2 * rows), seqs(dst, g, 0, rows), to),
                remote(kind + 1, g, lse.at[g + off_group, pl.ds(rows, rows)], ldst.at[g + off_group], to))

    def start_own(g):
        for kind in (0, 1, 2):
            q_copy(kind, g).start()

    def forward(g):
        q_copy(1, g).wait_recv()
        q_copy(2, g).wait_recv()
        for kind in (3, 4, 5):
            q_copy(kind, g).start()

    def forward_diagonal(g):
        q_copy(3, g).wait_recv()
        q_copy(6, g).start()

    def q_ready(g):
        for kind in (0, 4, 5, 6):
            q_copy(kind, g).wait_recv()

    def rs_start(stage, g):
        for copy in rs_copies(stage, g):
            copy.start()

    def rs_wait(stage, g):
        for copy in rs_copies(stage, g):
            copy.wait_recv()

    def kv_copy(b):
        slot = b % NBUF
        return pltpu.make_async_copy(c_ref.at[b], kv.at[slot], kv_sem.at[slot])

    for b in range(NBUF - 2):
        kv_copy(b).start()
    own = pltpu.make_async_copy(q_ref, qg.at[:, pl.ds(0, 8)], q_sem)
    own.start()

    barrier = pltpu.get_barrier_semaphore()
    for device in (partner, neighbour(0, True), neighbour(0, False)):
        pl.semaphore_signal(barrier, inc=1, device_id=device, device_id_type=MESH)
    pl.semaphore_wait(barrier, 3)
    own.wait()

    for g in range(AHEAD):
        start_own(g)
    forward(0)
    forward(1)
    forward_diagonal(0)

    lane = lax.broadcasted_iota(jnp.int32, (8 * 8, 128), 1)

    def combine(stage, pair):
        rows, ref, lref = ((32, r1, rl1), (16, r2, rl2), (8, r3, rl3))[stage]
        g = pair // PAIRS
        for u in range(2):
            b = 2 * pair + u
            j = b % G
            mine = lse[g, 0:rows]
            merged, total = merge(o[b, 0:rows], column(mine, lane[0:rows], j),
                                  ref[b], column(lref[g], lane[0:rows], j))
            if stage == 2:
                out_ref[jnp.maximum(b - 2 * off_pair, 0)] = merged
            else:
                o[b, 0:rows] = merged
                lse[g, 0:rows] = jnp.where(lane[0:rows] == j, total, mine)

    def attention(t):
        for u in range(2):
            b = 2 * t + u
            part, total = attend(qg[b], kv.at[b % NBUF], lens_ref[b], me, lora)
            o[b + 2 * off_pair] = part
            g = t // PAIRS + off_group
            lse[g] = jnp.where(lane == b % G, total, lse[g])

    def step(t, _):
        g = t // PAIRS

        @pl.when(t % PAIRS == 0)
        def _():
            @pl.when(g + AHEAD < n_groups)
            def _():
                start_own(g + AHEAD)

            @pl.when(g + 2 < n_groups)
            def _():
                forward(g + 2)

            @pl.when(g + 1 < n_groups)
            def _():
                forward_diagonal(g + 1)

            q_ready(g)

            @pl.when(g >= 1)
            def _():
                rs_start(0, g - 1)

        @pl.when(t % PAIRS == 2)
        def _():
            @pl.when(g >= 1)
            def _():
                rs_wait(0, g - 1)

            @pl.when(g >= 2)
            def _():
                rs_start(1, g - 2)

            @pl.when(g >= 3)
            def _():
                rs_wait(1, g - 3)

            @pl.when(g >= 4)
            def _():
                rs_start(2, g - 4)

            @pl.when(g >= 5)
            def _():
                rs_wait(2, g - 5)

        @pl.when(t + NBUF // 2 - 1 < n_pairs)
        def _():
            for u in range(2):
                kv_copy(2 * t + NBUF - 2 + u).start()
        for u in range(2):
            kv_copy(2 * t + u).wait()
        combine(0, t - LAG1 + off_pair)
        combine(1, t - LAG2 + off_pair)
        combine(2, t - LAG3 + off_pair)
        attention(t)
        return 0

    lax.fori_loop(0, n_pairs, step, 0)

    def combine_all(stage, lo, hi):
        def one(t, _):
            combine(stage, t + off_pair)
            return 0
        lax.fori_loop(lo, hi, one, 0)

    last = n_groups - 1
    rs_start(0, last)
    combine_all(0, n_pairs - LAG1, n_pairs - PAIRS)
    rs_start(1, last - 1)
    combine_all(1, n_pairs - LAG2, n_pairs - LAG2 + 2)
    rs_start(2, last - 3)
    rs_wait(1, last - 2)
    combine_all(1, n_pairs - 3 * PAIRS, n_pairs - 2 * PAIRS)
    rs_start(2, last - 2)
    rs_wait(0, last)
    combine_all(0, n_pairs - PAIRS, n_pairs)
    rs_start(1, last)
    rs_wait(2, last - 4)
    combine_all(2, n_pairs - LAG3, n_pairs - 4 * PAIRS)
    rs_wait(1, last - 1)
    combine_all(1, n_pairs - 2 * PAIRS, n_pairs - PAIRS)
    rs_start(2, last - 1)
    rs_wait(2, last - 3)
    combine_all(2, n_pairs - 4 * PAIRS, n_pairs - 3 * PAIRS)
    rs_wait(1, last)
    combine_all(1, n_pairs - PAIRS, n_pairs)
    rs_start(2, last)
    rs_wait(2, last - 2)
    combine_all(2, n_pairs - 3 * PAIRS, n_pairs - 2 * PAIRS)
    rs_wait(2, last - 1)
    combine_all(2, n_pairs - 2 * PAIRS, n_pairs - PAIRS)

    def sent(g, _):
        for kind in range(AG_KINDS):
            q_copy(kind, g).wait_send()
        for stage in range(3):
            for copy in rs_copies(stage, g):
                copy.wait_send()
        return 0

    lax.fori_loop(0, n_groups, sent, 0)
    rs_wait(2, last)
    combine_all(2, n_pairs - PAIRS, n_pairs)


def solution(mesh):
    def local(lens, q, cache):
        b, heads, k = q.shape
        r, page = cache.shape[1], cache.shape[3]
        lora = k - ROPE
        c = jnp.transpose(cache.reshape(b, r, page, k), (0, 2, 3, 1))
        groups = b // G
        off_group = (LAG3 + 2) // PAIRS
        pb = b + off_group * G
        pg = groups + off_group
        bf, f4 = jnp.bfloat16, jnp.float32
        kinds = AG_KINDS + RS_KINDS
        return pl.pallas_call(
            functools.partial(kernel, b, lora),
            out_shape=jax.ShapeDtypeStruct((b, heads, lora), bf),
            in_specs=[pl.BlockSpec(memory_space=pltpu.SMEM), pl.BlockSpec(memory_space=pl.ANY),
                      pl.BlockSpec(memory_space=pl.ANY)],
            out_specs=pl.BlockSpec(memory_space=pltpu.VMEM),
            scratch_shapes=[
                pltpu.VMEM((NBUF, page, k, r), bf),
                pltpu.VMEM((b, 8 * heads, k), bf),
                pltpu.VMEM((pb, 64, lora), bf), pltpu.VMEM((pg, 64, 128), f4),
                pltpu.VMEM((pb, 32, lora), bf), pltpu.VMEM((pg, 32, 128), f4),
                pltpu.VMEM((pb, 16, lora), bf), pltpu.VMEM((pg, 16, 128), f4),
                pltpu.VMEM((pb, 8, lora), bf), pltpu.VMEM((pg, 8, 128), f4),
                pltpu.SemaphoreType.DMA((NBUF,)), pltpu.SemaphoreType.DMA,
                pltpu.SemaphoreType.DMA((kinds, groups)), pltpu.SemaphoreType.DMA((kinds, groups)),
            ],
            compiler_params=pltpu.CompilerParams(collective_id=0, has_side_effects=True,
                                                 vmem_limit_bytes=64 * 2 ** 20 - 2 ** 16),
            name="decode",
        )(lens, q, c)

    f = jax.shard_map(local, mesh=mesh, in_specs=(P('dp'), P('dp', 'dcp', None), P('dp', None, 'dcp', None, None)),
                      out_specs=P('dp', 'dcp', None), check_vma=False)
    return lambda q, cache, lens: f(lens, q, cache)
```

time: 483 us -> 148 us (0.31); the launches traced: 478 us -> 148 us
  local copies, waits for them, and re-layouts: 208 us -> 5.19 us
  Pallas kernels: 0 us -> 143 us
  matrix products: 132 us -> 0 us
  waiting for transfers between devices: 93.7 us -> 0 us
  other arithmetic: 22.1 us -> 0 us
  between operations: 13.5 us -> 0.01 us
  starting transfers between devices: 8.06 us -> 0 us
    unnamed x4 -> x2, local copies, waits for them, and re-layouts: 200 us -> 5.19 us
    pallas_call x0 -> x1, Pallas kernels: none -> 143 us  [local(): pl.pallas_call(functools.partial(kernel, b, lora), out_shape=jax.ShapeDty...]
    dot_general x2 -> x0, matrix products: 132 us -> none  [the longest x1 77.1 us: local(): jnp.einsum('bhk,btk->bht', qa, c, preferred_element_type=jnp.float32)]
    all_to_all x2 -> x0, waiting for transfers between devices: 93.6 us -> none  [the longest x1 93.6 us: local(): od = lax.all_to_all(od.reshape(b, n, hl, lorav), 'dcp', 1, 1, tiled=True)]
    reduce_sum x3 -> x0, other arithmetic: 20 us -> none  [the longest x1 14.9 us: local(): l = jnp.sum(p, axis=2)]
    all_to_all x2 -> x0, starting transfers between devices: 8.06 us -> none  [the longest x1 4.28 us: local(): lse = lax.all_to_all(lse.reshape(b, n, hl), 'dcp', 1, 1, tiled=True)]
    reshape x1 -> x0, local copies, waits for them, and re-layouts: 7.41 us -> none  [local(): od = lax.all_to_all(od.reshape(b, n, hl, lorav), 'dcp', 1, 1, tiled=True)]
  transfers between devices with their start and end apart: 3 -> 0, of which waited for: 1 -> 0; matrix products, arithmetic and copies ran while one was open for 55% -> 0% of each run, Pallas kernels for 0% -> 0%
where the time goes in v1:
time: 148 us
  Pallas kernels  143 us (97%)
  local copies, waits for them, and re-layouts  5.19 us (4%)
    pallas_call x1, Pallas kernels, local(): pl.pallas_call(functools.partial(kernel, b, lora), out_shape=jax.ShapeDty...  143 us
    unnamed x2, local copies, waits for them, and re-layouts  5.19 us

profile of v1, /device:TPU:0, one launch (start us, length us, event | category | flops | bytes accessed | tf_op | source)
XLA Modules:
  0.0 147.9 jit_solution(17827708071247413816)
XLA Ops:
  0.0 2.9 %copy.4.q_ref = bf16[128,8,576]{2,1,0:T(8,128)(2,1)} copy(bf16[128,8,576]{0,2,1:T(8,128)(2,1)} %param.4) | data formatting | bytes 2359296 | tf_op args[0]
  2.9 142.7 %decode.1 = bf16[128,8,512]{2,1,0:T(8,128)(2,1)} custom-call(s32[128]{0:T(128)} %lens_ref.1, bf16[128,8,576]{2,1,0:T(8,128)(2,1)} %copy.4.q_ref, bf16[128,8,576,128]{3,2,1,0:T(8,128)(2,1)} %bitcast.1.c_ref), custom_call_target="tpu_custom_call" | custom-call | tf_op jit(solution)/shard_map/decode/pallas_call | solution.py:291
  145.6 2.3 %copy.6 = bf16[128,8,512]{2,1,0:T(8,128)(2,1)} copy(bf16[128,8,512]{2,1,0:T(8,128)(2,1)} %decode.1) | data formatting | bytes 2097152

commit v2 on v1

v2 whole, which is shorter than its diff:
```python
import functools

import jax
import jax.numpy as jnp
from jax import lax
from jax.experimental import pallas as pl
from jax.experimental.pallas import tpu as pltpu
from jax.sharding import PartitionSpec as P

ROPE = 64
QK_DIM = 192
SCALE = QK_DIM ** -0.5
MESH = pl.DeviceIdType.MESH

G = 8
W = 4
UNITS = G // W
AHEAD = 4
LAG1, LAG2, LAG3 = 4, 10, 16
OFF = 16
NBUF = 3 * W
TILE = 256
LOG2E = 1.4426950408889634
AG_KINDS, RS_KINDS = 14, 6


def scores(ql, r, c):
    lora = 2 * TILE
    heads, rope = r.shape

    def rows(p, lo, hi):
        return jnp.concatenate([c[2 * p, lo:hi], c[2 * p + 1, lo:hi]], axis=1)

    ql = jnp.concatenate([ql] * 2, axis=0)
    z = jnp.zeros((heads, rope), jnp.bfloat16)
    qr = jnp.concatenate([jnp.concatenate([r if i == p else z for i in range(4)], axis=1)
                          for p in range(4)], axis=0)
    cr = jnp.concatenate([rows(p, lora, lora + rope) for p in range(4)], axis=0)
    rotary = jnp.dot(qr, cr, preferred_element_type=jnp.float32)
    out = []
    for p in range(4):
        v = jnp.dot(ql, rows(p, 0, lora), preferred_element_type=jnp.float32)[:heads]
        v = v + rotary[heads * p:heads * (p + 1)]
        out += [v[:, :128], v[:, 128:]]
    return out


def values(p, c):
    lora = 2 * TILE
    o = None
    for i in range(4):
        both = jnp.concatenate([c[2 * i, :lora], c[2 * i + 1, :lora]], axis=1)
        x = lax.dot_general(p[i], both, (((1,), (1,)), ((), ())), preferred_element_type=jnp.float32)
        o = x if o is None else o + x
    return o.astype(jnp.bfloat16)


def softmax(s, length, d):
    lane = lax.broadcasted_iota(jnp.int32, s[0].shape, 1)
    s = [jnp.where(lane < lax.shift_right_arithmetic(length - 8 * d - i + 63, 6), v, -jnp.inf)
         for i, v in enumerate(s)]
    m = jnp.max(functools.reduce(jnp.maximum, s), axis=1, keepdims=True)
    m = jnp.where(m == -jnp.inf, 0.0, m)
    mc = m * (SCALE * LOG2E)
    p = [jnp.exp2(v * (SCALE * LOG2E) - mc) for v in s]
    l = jnp.sum(functools.reduce(jnp.add, p), axis=1, keepdims=True)
    has = l > 0.0
    safe = jnp.where(has, l, 1.0)
    r = jnp.where(has, 1.0 / safe, 0.0)
    lse = jnp.where(has, m * SCALE + jnp.log(safe), -jnp.inf)
    return [jnp.concatenate([p[2 * i] * r, p[2 * i + 1] * r], axis=1).astype(jnp.bfloat16) for i in range(4)], lse


def column(ref, lane, j):
    return jnp.max(jnp.where(lane == j, ref, -jnp.inf), axis=1, keepdims=True)


def merge(oa, la, ob, lb):
    top = jnp.maximum(la, lb)
    top = jnp.where(top == -jnp.inf, 0.0, top)
    wa, wb = jnp.exp(la - top), jnp.exp(lb - top)
    w = wa + wb
    has = w > 0.0
    safe = jnp.where(has, w, 1.0)
    inv = jnp.where(has, 1.0 / safe, 0.0)
    o = (wa * inv) * oa.astype(jnp.float32) + (wb * inv) * ob.astype(jnp.float32)
    return o.astype(jnp.bfloat16), jnp.where(has, top + jnp.log(safe), -jnp.inf)


def kernel(n_seq, lora, lens_ref, ql_ref, qr_ref, c_ref, out_ref, kv, ql, qr, prob, o, lse, r1, rl1, r2, rl2, r3, rl3,
           kv_sem, q_sem, send_sem, recv_sem):
    n_groups, n_units = n_seq // G, n_seq // W
    off_group = OFF // UNITS
    me = lax.axis_index("dcp")
    dp = lax.axis_index("dp")
    y, x, core = me // 4, (me // 2) % 2, me % 2
    partner = (dp, y * 4 + x * 2 + (1 - core))

    def neighbour(g, first):
        par = g % 2 if first else (g + 1) % 2
        return (dp, ((y + par) % 2) * 4 + ((x + 1 - par) % 2) * 2 + core)

    def remote(kind, g, src, dst, device):
        return pltpu.make_async_remote_copy(
            src_ref=src, dst_ref=dst, send_sem=send_sem.at[kind, g], recv_sem=recv_sem.at[kind, g],
            device_id=device, device_id_type=MESH)

    def q_blocks(g, block):
        return (ql.at[pl.ds(g * G, G), pl.ds(block * 8, 8)], qr.at[pl.ds(g * G // 2, G // 2), pl.ds(block * 8, 8)])

    def q_copies(kind, g):
        src, dst, to = ((0, 4, partner), (0, 2, neighbour(g, True)), (0, 1, neighbour(g, False)),
                        (2, 3, neighbour(g, False)), (2, 6, partner), (1, 5, partner), (3, 7, partner))[kind]
        return [remote(2 * kind + i, g, q_blocks(g, src)[i], q_blocks(g, dst)[i], to) for i in range(2)]

    def seqs(ref, g, lo, hi):
        return ref.at[pl.ds((g + off_group) * G, G), pl.ds(lo, hi - lo)]

    def rs_copies(stage, g):
        rows, dst, ldst, to = ((32, r1, rl1, partner), (16, r2, rl2, neighbour(g, True)),
                               (8, r3, rl3, neighbour(g, False)))[stage]
        kind = AG_KINDS + 2 * stage
        return (remote(kind, g, seqs(o, g, rows, 2 * rows), seqs(dst, g, 0, rows), to),
                remote(kind + 1, g, lse.at[g + off_group, pl.ds(rows, rows)], ldst.at[g + off_group], to))

    def q_start(kinds, g):
        for kind in kinds:
            for copy in q_copies(kind, g):
                copy.start()

    def q_wait(kinds, g):
        for kind in kinds:
            for copy in q_copies(kind, g):
                copy.wait_recv()

    def start_own(g):
        q_start((1, 2, 0), g)

    def forward(g):
        q_wait((1, 2), g)
        q_start((3, 4, 5), g)

    def forward_diagonal(g):
        q_wait((3,), g)
        q_start((6,), g)

    def q_ready(g):
        q_wait((0, 4, 5, 6), g)

    def rs_start(stage, g):
        for copy in rs_copies(stage, g):
            copy.start()

    def rs_wait(stage, g):
        for copy in rs_copies(stage, g):
            copy.wait_recv()

    def kv_copy(b):
        slot = b % NBUF
        return pltpu.make_async_copy(c_ref.at[b], kv.at[slot], kv_sem.at[slot])

    def own_copies(lo, hi, k):
        return (pltpu.make_async_copy(ql_ref.at[lo:hi], ql.at[lo:hi, 0:8], q_sem.at[k]),
                pltpu.make_async_copy(qr_ref.at[lo // 2:hi // 2], qr.at[lo // 2:hi // 2, 0:8], q_sem.at[k + 1]))

    first_own, other_own = own_copies(0, 2 * G, 0), own_copies(2 * G, n_seq, 2)
    for copy in first_own + other_own:
        copy.start()
    for b in range(W):
        kv_copy(b).start()

    barrier = pltpu.get_barrier_semaphore()
    for device in (partner, neighbour(0, True), neighbour(0, False)):
        pl.semaphore_signal(barrier, inc=1, device_id=device, device_id_type=MESH)
    pl.semaphore_wait(barrier, 3)
    for copy in first_own:
        copy.wait()
    start_own(0)
    start_own(1)
    for copy in other_own:
        copy.wait()
    forward(0)
    start_own(2)
    forward(1)
    forward_diagonal(0)
    start_own(3)

    lane = lax.broadcasted_iota(jnp.int32, (8 * 8, 128), 1)

    def combine(stage, unit):
        rows, ref, lref = ((32, r1, rl1), (16, r2, rl2), (8, r3, rl3))[stage]
        g = unit // UNITS
        mine = lse[g, 0:rows]
        theirs = lref[g]
        for u in range(W):
            b = W * unit + u
            j = b % G
            merged, total = merge(o[b, 0:rows], column(mine, lane[0:rows], j),
                                  ref[b], column(theirs, lane[0:rows], j))
            if stage == 2:
                out_ref[jnp.maximum(b - W * OFF, 0)] = merged
            else:
                o[b, 0:rows] = merged
                mine = jnp.where(lane[0:rows] == j, total, mine)
        if stage != 2:
            lse[g, 0:rows] = mine

    def finish(t):
        for j in range(W):
            b = W * t + j
            o[b + W * OFF] = values([prob[(t + 2) % 2, j, i] for i in range(4)], kv.at[(b + NBUF) % NBUF])

    def begin(t):
        rows = lse[t // UNITS + off_group]
        for j in range(W):
            b = W * t + j
            p, total = softmax(scores(ql[b], qr[W // 2 * t + j % (W // 2), :, ROPE * (j // (W // 2)):ROPE * (j // (W // 2) + 1)],
                                      kv.at[b % NBUF]), lens_ref[b], me)
            for i in range(4):
                prob[t % 2, j, i] = p[i]
            rows = jnp.where(lane == b % G, total, rows)
        lse[t // UNITS + off_group] = rows

    def step(t, _):
        g = t // UNITS

        @pl.when(t % UNITS == 0)
        def _():
            @pl.when(g + AHEAD < n_groups)
            def _():
                start_own(g + AHEAD)

            @pl.when(g + 2 < n_groups)
            def _():
                forward(g + 2)

            @pl.when(g + 1 < n_groups)
            def _():
                forward_diagonal(g + 1)

            q_ready(g)

            @pl.when(g >= 2)
            def _():
                rs_wait(0, g - 2)

            @pl.when(g >= 3)
            def _():
                rs_start(1, g - 3)

            @pl.when(g >= 5)
            def _():
                rs_wait(1, g - 5)

            @pl.when(g >= 6)
            def _():
                rs_start(2, g - 6)

            @pl.when(g >= 8)
            def _():
                rs_wait(2, g - 8)

        @pl.when((t % UNITS == 1) & (g >= 1))
        def _():
            rs_start(0, g - 1)

        @pl.when(t + 1 < n_units)
        def _():
            for j in range(W):
                kv_copy(W * (t + 1) + j).start()
        for j in range(W):
            kv_copy(W * t + j).wait()
        combine(0, t - LAG1 + OFF)
        combine(1, t - LAG2 + OFF)
        combine(2, t - LAG3 + OFF)
        begin(t)
        finish(t - 1)
        return 0

    lax.fori_loop(0, n_units, step, 0)

    def combine_all(stage, lo, hi):
        def one(t, _):
            combine(stage, t + OFF)
            return 0
        lax.fori_loop(lo, hi, one, 0)

    last = n_groups - 1

    def merge_group(stage, g):
        rs_wait(stage, g)
        combine_all(stage, UNITS * g, UNITS * (g + 1))
        if stage < 2:
            rs_start(stage + 1, g)

    rs_start(1, last - 2)
    rs_start(2, last - 5)
    finish(n_units - 1)
    rs_start(0, last)
    for stage, back in ((1, 4), (0, 1), (1, 3), (0, 0), (2, 7), (1, 2), (2, 6), (2, 5), (1, 1), (2, 4), (2, 3), (1, 0),
                        (2, 2), (2, 1)):
        merge_group(stage, last - back)

    def sent(g, _):
        for kind in range(AG_KINDS // 2):
            for copy in q_copies(kind, g):
                copy.wait_send()
        for stage in range(3):
            for copy in rs_copies(stage, g):
                copy.wait_send()
        return 0

    lax.fori_loop(0, n_groups, sent, 0)
    merge_group(2, last)


def solution(mesh):
    def local(lens, q, cache):
        b, heads, k = q.shape
        r, page = cache.shape[1], cache.shape[3]
        lora = k - ROPE
        c = jnp.transpose(cache.reshape(b, r, page, k), (0, 2, 3, 1))
        groups = b // G
        q_latent = q[:, :, :lora]
        q_rotary = q[:, :, lora:].reshape(b // W, 2, W // 2, heads, ROPE).transpose(0, 2, 3, 1, 4)
        q_rotary = q_rotary.reshape(b // 2, heads, 2 * ROPE)
        pb = b + OFF * W
        pg = groups + OFF // UNITS
        bf, f4 = jnp.bfloat16, jnp.float32
        kinds = AG_KINDS + RS_KINDS
        return pl.pallas_call(
            functools.partial(kernel, b, lora),
            out_shape=jax.ShapeDtypeStruct((b, heads, lora), bf),
            in_specs=[pl.BlockSpec(memory_space=pltpu.SMEM)] + [pl.BlockSpec(memory_space=pl.ANY)] * 3,
            out_specs=pl.BlockSpec(memory_space=pltpu.VMEM),
            scratch_shapes=[
                pltpu.VMEM((NBUF, page, k, r), bf),
                pltpu.VMEM((b, 8 * heads, lora), bf), pltpu.VMEM((b // 2, 8 * heads, 2 * ROPE), bf),
                pltpu.VMEM((2, W, 4, 64, TILE), bf),
                pltpu.VMEM((pb, 64, lora), bf), pltpu.VMEM((pg, 64, 128), f4),
                pltpu.VMEM((pb, 32, lora), bf), pltpu.VMEM((pg, 32, 128), f4),
                pltpu.VMEM((pb, 16, lora), bf), pltpu.VMEM((pg, 16, 128), f4),
                pltpu.VMEM((pb, 8, lora), bf), pltpu.VMEM((pg, 8, 128), f4),
                pltpu.SemaphoreType.DMA((NBUF,)), pltpu.SemaphoreType.DMA((4,)),
                pltpu.SemaphoreType.DMA((kinds, groups)), pltpu.SemaphoreType.DMA((kinds, groups)),
            ],
            compiler_params=pltpu.CompilerParams(collective_id=0, has_side_effects=True,
                                                 vmem_limit_bytes=64 * 2 ** 20 - 2 ** 16),
            name="decode",
        )(lens, q_latent, q_rotary, c)

    f = jax.shard_map(local, mesh=mesh, in_specs=(P('dp'), P('dp', 'dcp', None), P('dp', None, 'dcp', None, None)),
                      out_specs=P('dp', 'dcp', None), check_vma=False)
    return lambda q, cache, lens: f(lens, q, cache)
```

time: 148 us -> 125 us (0.84)
  Pallas kernels: 143 us -> 117 us
  local copies, waits for them, and re-layouts: 5.19 us -> 7.35 us
    pallas_call x1, Pallas kernels: 143 us -> 117 us  [local(): pl.pallas_call(functools.partial(kernel, b, lora), out_shape=jax.ShapeDty...]
    slice x0 -> x2, local copies, waits for them, and re-layouts: none -> 2.21 us  [the longest x1 1.29 us: local(): q_latent = q[:, :, :lora]]
    unnamed x2 -> x3, local copies, waits for them, and re-layouts: 5.19 us -> 4.14 us
where the time goes in v2:
time: 125 us
  Pallas kernels  117 us (94%)
  local copies, waits for them, and re-layouts  7.35 us (6%)
    pallas_call x1, Pallas kernels, local(): pl.pallas_call(functools.partial(kernel, b, lora), out_shape=jax.ShapeDty...  117 us
    unnamed x3, local copies, waits for them, and re-layouts  4.14 us

profile of v2, /device:TPU:0, one launch (start us, length us, event | category | flops | bytes accessed | tf_op | source)
XLA Modules:
  0.0 124.7 jit_solution(16243137802753249002)
XLA Ops:
  0.0 0.9 slice.7
  0.9 0.2 copy.10
  1.1 0.2 copy.8
  1.3 0.8 reshape.10.qr_ref
  2.1 1.3 %slice.6 = bf16[128,8,512]{0,2,1:T(8,128)(2,1)S(1)} slice(bf16[128,8,576]{0,2,1:T(8,128)(2,1)} %param.4), slice={[0:128], [0:8], [0:512]} | slice | bytes 2097152 | tf_op jit(solution)/shard_map/slice | solution.py:324
  3.4 1.7 %copy.9.ql_ref = bf16[128,8,512]{2,1,0:T(8,128)(2,1)} copy(bf16[128,8,512]{0,2,1:T(8,128)(2,1)S(1)} %slice.6) | data formatting | bytes 2097152
  5.1 117.3 %decode.1 = bf16[128,8,512]{2,1,0:T(8,128)(2,1)} custom-call(s32[128]{0:T(128)} %lens_ref.1, bf16[128,8,512]{2,1,0:T(8,128)(2,1)} %copy.9.ql_ref, bf16[64,8,128]{2,1,0:T(8,128)(2,1)} %reshape.10.qr_ref, bf16[128,8,576,128]{3,2,1,0:T(8,128)(2,1)} %bitcast.3.c_ref), custom_call_target="tpu_custom_call" | custom-call | tf_op jit(solution)/shard_map/decode/pallas_call | solution.py:331
  122.4 2.3 %copy.12 = bf16[128,8,512]{2,1,0:T(8,128)(2,1)} copy(bf16[128,8,512]{2,1,0:T(8,128)(2,1)} %decode.1) | data formatting | bytes 2097152

commit v3 on v2

--- a/solution.py
+++ b/solution.py
@@ -16,8 +16,9 @@
 W = 4
 UNITS = G // W
 AHEAD = 4
-LAG1, LAG2, LAG3 = 4, 10, 16
-OFF = 16
+LAGS = (4, 9, 14)
+TAIL = (4, 7, 10)
+OFF = 14
 NBUF = 3 * W
 TILE = 256
 LOG2E = 1.4426950408889634
@@ -50,9 +51,9 @@
     o = None
     for i in range(4):
         both = jnp.concatenate([c[2 * i, :lora], c[2 * i + 1, :lora]], axis=1)
-        x = lax.dot_general(p[i], both, (((1,), (1,)), ((), ())), preferred_element_type=jnp.float32)
+        x = lax.dot_general(both, p[i], (((1,), (1,)), ((), ())), preferred_element_type=jnp.float32)
         o = x if o is None else o + x
-    return o.astype(jnp.bfloat16)
+    return o.astype(jnp.bfloat16).T
 
 
 def softmax(s, length, d):
@@ -87,7 +88,7 @@
     return o.astype(jnp.bfloat16), jnp.where(has, top + jnp.log(safe), -jnp.inf)
 
 
-def kernel(n_seq, lora, lens_ref, ql_ref, qr_ref, c_ref, out_ref, kv, ql, qr, prob, o, lse, r1, rl1, r2, rl2, r3, rl3,
+def kernel(n_seq, lora, lens_ref, q_ref, c_ref, out_ref, kv, own, ql, qr, prob, o, lse, r1, rl1, r2, rl2, r3, rl3,
            kv_sem, q_sem, send_sem, recv_sem):
     n_groups, n_units = n_seq // G, n_seq // W
     off_group = OFF // UNITS
@@ -95,6 +96,7 @@
     dp = lax.axis_index("dp")
     y, x, core = me // 4, (me // 2) % 2, me % 2
     partner = (dp, y * 4 + x * 2 + (1 - core))
+    diagonal = (dp, (1 - y) * 4 + (1 - x) * 2 + core)
 
     def neighbour(g, first):
         par = g % 2 if first else (g + 1) % 2
@@ -133,12 +135,24 @@
             for copy in q_copies(kind, g):
                 copy.wait_recv()
 
+    def pack(g):
+        for j in range(G):
+            ql[g * G + j, 0:8] = own[g * G + j, :, 0:lora]
+        for i in range(G // 2):
+            b = g * G + i // (W // 2) * W + i % (W // 2)
+            qr[g * G // 2 + i, 0:8] = jnp.concatenate([own[b, :, lora:], own[b + W // 2, :, lora:]], axis=1)
+
     def start_own(g):
+        pack(g)
         q_start((1, 2, 0), g)
 
-    def forward(g):
+    def start_diagonal(g):
+        for i in range(2):
+            remote(6 + i, g, q_blocks(g, 0)[i], q_blocks(g, 3)[i], diagonal).start()
+
+    def forward(g, kinds=(3, 4, 5)):
         q_wait((1, 2), g)
-        q_start((3, 4, 5), g)
+        q_start(kinds, g)
 
     def forward_diagonal(g):
         q_wait((3,), g)
@@ -159,27 +173,23 @@
         slot = b % NBUF
         return pltpu.make_async_copy(c_ref.at[b], kv.at[slot], kv_sem.at[slot])
 
-    def own_copies(lo, hi, k):
-        return (pltpu.make_async_copy(ql_ref.at[lo:hi], ql.at[lo:hi, 0:8], q_sem.at[k]),
-                pltpu.make_async_copy(qr_ref.at[lo // 2:hi // 2], qr.at[lo // 2:hi // 2, 0:8], q_sem.at[k + 1]))
-
-    first_own, other_own = own_copies(0, 2 * G, 0), own_copies(2 * G, n_seq, 2)
-    for copy in first_own + other_own:
-        copy.start()
+    first_own = pltpu.make_async_copy(q_ref.at[0:2 * G], own.at[0:2 * G], q_sem.at[0])
+    other_own = pltpu.make_async_copy(q_ref.at[2 * G:n_seq], own.at[2 * G:n_seq], q_sem.at[1])
+    first_own.start()
+    other_own.start()
     for b in range(W):
         kv_copy(b).start()
 
     barrier = pltpu.get_barrier_semaphore()
-    for device in (partner, neighbour(0, True), neighbour(0, False)):
+    for device in (partner, diagonal, neighbour(0, True), neighbour(0, False)):
         pl.semaphore_signal(barrier, inc=1, device_id=device, device_id_type=MESH)
-    pl.semaphore_wait(barrier, 3)
-    for copy in first_own:
-        copy.wait()
+    pl.semaphore_wait(barrier, 4)
+    first_own.wait()
     start_own(0)
+    start_diagonal(0)
     start_own(1)
-    for copy in other_own:
-        copy.wait()
-    forward(0)
+    other_own.wait()
+    forward(0, (4, 5))
     start_own(2)
     forward(1)
     forward_diagonal(0)
@@ -187,12 +197,13 @@
 
     lane = lax.broadcasted_iota(jnp.int32, (8 * 8, 128), 1)
 
-    def combine(stage, unit):
+    def combine(stage, unit, count=1):
         rows, ref, lref = ((32, r1, rl1), (16, r2, rl2), (8, r3, rl3))[stage]
         g = unit // UNITS
         mine = lse[g, 0:rows]
+        totals = mine
         theirs = lref[g]
-        for u in range(W):
+        for u in range(W * count):
             b = W * unit + u
             j = b % G
             merged, total = merge(o[b, 0:rows], column(mine, lane[0:rows], j),
@@ -201,9 +212,9 @@
                 out_ref[jnp.maximum(b - W * OFF, 0)] = merged
             else:
                 o[b, 0:rows] = merged
-                mine = jnp.where(lane[0:rows] == j, total, mine)
+                totals = jnp.where(lane[0:rows] == j, total, totals)
         if stage != 2:
-            lse[g, 0:rows] = mine
+            lse[g, 0:rows] = totals
 
     def finish(t):
         for j in range(W):
@@ -224,8 +235,33 @@
     def step(t, _):
         g = t // UNITS
 
+        def exchange(parity):
+            for stage in (1, 0):
+                if LAGS[stage] % UNITS == parity:
+                    older = LAGS[stage] // UNITS + 1
+
+                    @pl.when(g >= older)
+                    def _(stage=stage, older=older):
+                        rs_start(stage + 1, g - older)
+            for stage in range(3):
+                if LAGS[stage] % UNITS == parity:
+                    back = LAGS[stage] // UNITS
+
+                    @pl.when(g >= back)
+                    def _(stage=stage, back=back):
+                        rs_wait(stage, g - back)
+
         @pl.when(t % UNITS == 0)
         def _():
+            q_ready(g)
+            exchange(0)
+
+        @pl.when(t % UNITS == 1)
+        def _():
+            @pl.when(g >= 1)
+            def _():
+                rs_start(0, g - 1)
+
             @pl.when(g + AHEAD < n_groups)
             def _():
                 start_own(g + AHEAD)
@@ -238,31 +274,7 @@
             def _():
                 forward_diagonal(g + 1)
 
-            q_ready(g)
-
-            @pl.when(g >= 2)
-            def _():
-                rs_wait(0, g - 2)
-
-            @pl.when(g >= 3)
-            def _():
-                rs_start(1, g - 3)
-
-            @pl.when(g >= 5)
-            def _():
-                rs_wait(1, g - 5)
-
-            @pl.when(g >= 6)
-            def _():
-                rs_start(2, g - 6)
-
-            @pl.when(g >= 8)
-            def _():
-                rs_wait(2, g - 8)
-
-        @pl.when((t % UNITS == 1) & (g >= 1))
-        def _():
-            rs_start(0, g - 1)
+            exchange(1)
 
         @pl.when(t + 1 < n_units)
         def _():
@@ -270,9 +282,8 @@
                 kv_copy(W * (t + 1) + j).start()
         for j in range(W):
             kv_copy(W * t + j).wait()
-        combine(0, t - LAG1 + OFF)
-        combine(1, t - LAG2 + OFF)
-        combine(2, t - LAG3 + OFF)
+        for stage in range(3):
+            combine(stage, t - LAGS[stage] + OFF)
         begin(t)
         finish(t - 1)
         return 0
@@ -286,20 +297,26 @@
         lax.fori_loop(lo, hi, one, 0)
 
     last = n_groups - 1
+    rest = []
+    for stage in range(3):
+        unit = n_units - LAGS[stage]
+        if unit % UNITS:
+            combine_all(stage, unit, unit + 1)
+        g = unit // UNITS - (unit % UNITS == 0)
+        if stage < 2:
+            rs_start(stage + 1, g)
+        rest += [(UNITS * i + TAIL[stage], stage, i) for i in range(g + 1, n_groups)]
 
     def merge_group(stage, g):
         rs_wait(stage, g)
-        combine_all(stage, UNITS * g, UNITS * (g + 1))
+        combine(stage, UNITS * g + OFF, UNITS)
         if stage < 2:
             rs_start(stage + 1, g)
 
-    rs_start(1, last - 2)
-    rs_start(2, last - 5)
     finish(n_units - 1)
     rs_start(0, last)
-    for stage, back in ((1, 4), (0, 1), (1, 3), (0, 0), (2, 7), (1, 2), (2, 6), (2, 5), (1, 1), (2, 4), (2, 3), (1, 0),
-                        (2, 2), (2, 1)):
-        merge_group(stage, last - back)
+    for _, stage, g in sorted(rest)[:-1]:
+        merge_group(stage, g)
 
     def sent(g, _):
         for kind in range(AG_KINDS // 2):
@@ -321,9 +338,6 @@
         lora = k - ROPE
         c = jnp.transpose(cache.reshape(b, r, page, k), (0, 2, 3, 1))
         groups = b // G
-        q_latent = q[:, :, :lora]
-        q_rotary = q[:, :, lora:].reshape(b // W, 2, W // 2, heads, ROPE).transpose(0, 2, 3, 1, 4)
-        q_rotary = q_rotary.reshape(b // 2, heads, 2 * ROPE)
         pb = b + OFF * W
         pg = groups + OFF // UNITS
         bf, f4 = jnp.bfloat16, jnp.float32
@@ -331,23 +345,24 @@
         return pl.pallas_call(
             functools.partial(kernel, b, lora),
             out_shape=jax.ShapeDtypeStruct((b, heads, lora), bf),
-            in_specs=[pl.BlockSpec(memory_space=pltpu.SMEM)] + [pl.BlockSpec(memory_space=pl.ANY)] * 3,
+            in_specs=[pl.BlockSpec(memory_space=pltpu.SMEM)] + [pl.BlockSpec(memory_space=pl.ANY)] * 2,
             out_specs=pl.BlockSpec(memory_space=pltpu.VMEM),
             scratch_shapes=[
                 pltpu.VMEM((NBUF, page, k, r), bf),
+                pltpu.VMEM((b, heads, k), bf),
                 pltpu.VMEM((b, 8 * heads, lora), bf), pltpu.VMEM((b // 2, 8 * heads, 2 * ROPE), bf),
                 pltpu.VMEM((2, W, 4, 64, TILE), bf),
                 pltpu.VMEM((pb, 64, lora), bf), pltpu.VMEM((pg, 64, 128), f4),
                 pltpu.VMEM((pb, 32, lora), bf), pltpu.VMEM((pg, 32, 128), f4),
                 pltpu.VMEM((pb, 16, lora), bf), pltpu.VMEM((pg, 16, 128), f4),
                 pltpu.VMEM((pb, 8, lora), bf), pltpu.VMEM((pg, 8, 128), f4),
-                pltpu.SemaphoreType.DMA((NBUF,)), pltpu.SemaphoreType.DMA((4,)),
+                pltpu.SemaphoreType.DMA((NBUF,)), pltpu.SemaphoreType.DMA((2,)),
                 pltpu.SemaphoreType.DMA((kinds, groups)), pltpu.SemaphoreType.DMA((kinds, groups)),
             ],
             compiler_params=pltpu.CompilerParams(collective_id=0, has_side_effects=True,
                                                  vmem_limit_bytes=64 * 2 ** 20 - 2 ** 16),
             name="decode",
-        )(lens, q_latent, q_rotary, c)
+        )(lens, q, c)
 
     f = jax.shard_map(local, mesh=mesh, in_specs=(P('dp'), P('dp', 'dcp', None), P('dp', None, 'dcp', None, None)),
                       out_specs=P('dp', 'dcp', None), check_vma=False)

time: 125 us -> 117 us (0.936)
  Pallas kernels: 117 us -> 111 us
  local copies, waits for them, and re-layouts: 7.35 us -> 5.19 us
    pallas_call x1, Pallas kernels: 117 us -> 111 us  [local(): pl.pallas_call(functools.partial(kernel, b, lora), out_shape=jax.ShapeDty...]
    slice x2 -> x0, local copies, waits for them, and re-layouts: 2.21 us -> none  [the longest x1 1.29 us: local(): q_latent = q[:, :, :lora]]
    unnamed x3 -> x2, local copies, waits for them, and re-layouts: 4.14 us -> 5.19 us
where the time goes in v3:
time: 117 us
  Pallas kernels  111 us (95%)
  local copies, waits for them, and re-layouts  5.19 us (4%)
    pallas_call x1, Pallas kernels, local(): pl.pallas_call(functools.partial(kernel, b, lora), out_shape=jax.ShapeDty...  111 us
    unnamed x2, local copies, waits for them, and re-layouts  5.19 us

profile of v3, /device:TPU:0, one launch (start us, length us, event | category | flops | bytes accessed | tf_op | source)
XLA Modules:
  0.0 116.6 jit_solution(12978013997451867781)
XLA Ops:
  0.0 2.9 %copy.4.q_ref = bf16[128,8,576]{2,1,0:T(8,128)(2,1)} copy(bf16[128,8,576]{0,2,1:T(8,128)(2,1)} %param.4) | data formatting | bytes 2359296 | tf_op args[0]
  2.9 111.4 %decode.1 = bf16[128,8,512]{2,1,0:T(8,128)(2,1)} custom-call(s32[128]{0:T(128)} %lens_ref.1, bf16[128,8,576]{2,1,0:T(8,128)(2,1)} %copy.4.q_ref, bf16[128,8,576,128]{3,2,1,0:T(8,128)(2,1)} %bitcast.1.c_ref), custom_call_target="tpu_custom_call" | custom-call | tf_op jit(solution)/shard_map/decode/pallas_call | solution.py:345
  114.3 2.3 %copy.6 = bf16[128,8,512]{2,1,0:T(8,128)(2,1)} copy(bf16[128,8,512]{2,1,0:T(8,128)(2,1)} %decode.1) | data formatting | bytes 2097152

commit v4 on v3

--- a/solution.py
+++ b/solution.py
@@ -15,7 +15,7 @@
 G = 8
 W = 4
 UNITS = G // W
-AHEAD = 4
+AHEAD = 6
 LAGS = (4, 9, 14)
 TAIL = (4, 7, 10)
 OFF = 14
@@ -194,6 +194,8 @@
     forward(1)
     forward_diagonal(0)
     start_own(3)
+    start_own(4)
+    start_own(5)
 
     lane = lax.broadcasted_iota(jnp.int32, (8 * 8, 128), 1)
 
@@ -235,6 +237,11 @@
     def step(t, _):
         g = t // UNITS
 
+        @pl.when(t + 1 < n_units)
+        def _():
+            for j in range(W):
+                kv_copy(W * (t + 1) + j).start()
+
         def exchange(parity):
             for stage in (1, 0):
                 if LAGS[stage] % UNITS == parity:
@@ -276,10 +283,6 @@
 
             exchange(1)
 
-        @pl.when(t + 1 < n_units)
-        def _():
-            for j in range(W):
-                kv_copy(W * (t + 1) + j).start()
         for j in range(W):
             kv_copy(W * t + j).wait()
         for stage in range(3):

time: 117 us -> 116 us (level)
  no operation moved by 1% of the time
where the time goes in v4:
time: 116 us
  Pallas kernels  110 us (95%)
  local copies, waits for them, and re-layouts  5.19 us (4%)
    pallas_call x1, Pallas kernels, local(): pl.pallas_call(functools.partial(kernel, b, lora), out_shape=jax.ShapeDty...  110 us
    unnamed x2, local copies, waits for them, and re-layouts  5.19 us

profile of v4, /device:TPU:0, one launch (start us, length us, event | category | flops | bytes accessed | tf_op | source)
XLA Modules:
  0.0 115.6 jit_solution(12451787615593953905)
XLA Ops:
  0.0 2.9 %copy.4.q_ref = bf16[128,8,576]{2,1,0:T(8,128)(2,1)} copy(bf16[128,8,576]{0,2,1:T(8,128)(2,1)} %param.4) | data formatting | bytes 2359296 | tf_op args[0]
  2.9 110.4 %decode.1 = bf16[128,8,512]{2,1,0:T(8,128)(2,1)} custom-call(s32[128]{0:T(128)} %lens_ref.1, bf16[128,8,576]{2,1,0:T(8,128)(2,1)} %copy.4.q_ref, bf16[128,8,576,128]{3,2,1,0:T(8,128)(2,1)} %bitcast.1.c_ref), custom_call_target="tpu_custom_call" | custom-call | tf_op jit(solution)/shard_map/decode/pallas_call | solution.py:348
  113.3 2.3 %copy.6 = bf16[128,8,512]{2,1,0:T(8,128)(2,1)} copy(bf16[128,8,512]{2,1,0:T(8,128)(2,1)} %decode.1) | data formatting | bytes 2097152
